TPU v7x, 32 devices: a whole 2x2x4 slice. The times are simulated.
32 devices in a mesh: ta: 1, gx: 8 (over y, x, core), gy: 4 (over z).
Axes of the slice: x: 2, y: 2, z: 4, core: 2. Of those that a mesh axis runs over, the one named last changes fastest.
Arguments:
- propagator: bfloat16 [1, 2, 4, 3, 4, 3, 64, 4096], P('ta', None, None, None, None, None, 'gx', 'gy'), may hold values from -1.5 to 1.5
- gamma_table: int32 [16, 8], replicated, may hold values from 0 to 3, as said below
Outputs:
- spectrum: float32 [1, 16, 64, 64, 128], P('ta', None, ('gx', 'gy'))
Inputs may be any that keep to these rules, and one draw needn't show every extreme that they name: gamma_table[g, 0:4] is a permutation of 0 to 3, gamma_table[g, 4:8] are powers of i.
All inputs are finite; a program needn't handle non-finite values.
Results may differ from a plain program's by a relative error of at most 0.0061.
Values may be sent and summed in bfloat16 or wider, within the bound.
No kernel may reach another device: no remote copies, remote signals or barrier semaphores. Data moves between devices by JAX's collectives and lax.ppermute only.
A program may use at most 192 MiB of HBM per device.

v0:
```python
import math

import jax
import jax.numpy as jnp
from jax import lax
from jax.sharding import PartitionSpec as P

EXTENT = 64


def channel_weights(channel_table):
    spin_index = jnp.arange(4, dtype=jnp.int32)
    targets = channel_table[:, :4]
    codes_all = channel_table[:, 4:]
    mapping = (targets[:, :, None] == spin_index[None, None, :]).astype(jnp.float32)
    phase_real = (codes_all == 0).astype(jnp.float32) - (codes_all == 2).astype(jnp.float32)
    phase_imag = (codes_all == 1).astype(jnp.float32) - (codes_all == 3).astype(jnp.float32)
    pair_real = (
        phase_real[:, None, :] * phase_real[:, :, None]
        - phase_imag[:, None, :] * phase_imag[:, :, None]
    )
    pair_imag = (
        phase_real[:, None, :] * phase_imag[:, :, None]
        + phase_imag[:, None, :] * phase_real[:, :, None]
    )
    source_map = jnp.transpose(mapping, (0, 2, 1))
    selector = source_map[:, :, None, :, None] * mapping[:, None, :, None, :]
    count_channels = channel_table.shape[0]
    weight_real = (pair_real[:, None, :, :, None] * selector).reshape(count_channels, 256)
    weight_imag = (pair_imag[:, None, :, :, None] * selector).reshape(count_channels, 256)
    return (weight_real, weight_imag)


def spin_products(field_real, field_imag):
    site_count = field_real.shape[-1]
    total_real = jnp.zeros((4, 4, 4, 4, site_count), jnp.float32)
    total_imag = jnp.zeros((4, 4, 4, 4, site_count), jnp.float32)
    for color_in in range(3):
        for color_out in range(3):
            left_real = field_real[:, color_in, :, color_out].astype(jnp.float32)
            left_imag = field_imag[:, color_in, :, color_out].astype(jnp.float32)
            total_real = (
                total_real
                + left_real[:, :, None, None] * left_real[None, None]
                + left_imag[:, :, None, None] * left_imag[None, None]
            )
            total_imag = (
                total_imag
                + left_imag[:, :, None, None] * left_real[None, None]
                - left_real[:, :, None, None] * left_imag[None, None]
            )
    return (total_real.reshape(256, site_count), total_imag.reshape(256, site_count))


def dft_tables(length):
    steps_index = lax.iota(jnp.int32, length)
    phases = steps_index[:, None] * steps_index[None, :] % length
    angles = phases.astype(jnp.float32) * (2.0 * math.pi / length)
    norm_factor = 1.0 / math.sqrt(length)
    return (
        (jnp.cos(angles) * norm_factor).astype(jnp.bfloat16),
        (jnp.sin(angles) * norm_factor).astype(jnp.bfloat16),
    )


def transform(complex_pair, which_axis, out_type, cosine, sine_table):
    field_real, field_imag = complex_pair

    def contract_axis(values, weights):
        moved = jnp.tensordot(
            values, weights, axes=([which_axis], [0]), preferred_element_type=jnp.float32
        )
        return jnp.moveaxis(moved, -1, which_axis)

    new_real = contract_axis(field_real, cosine) + contract_axis(field_imag, sine_table)
    new_imag = contract_axis(field_imag, cosine) - contract_axis(field_real, sine_table)
    return (new_real.astype(out_type), new_imag.astype(out_type))


def body(propagator, gamma_table):
    weight_real, weight_imag = channel_weights(gamma_table)
    stack_real = jnp.concatenate([weight_real, -weight_imag], axis=1).astype(jnp.bfloat16)
    stack_imag = jnp.concatenate([weight_imag, weight_real], axis=1).astype(jnp.bfloat16)
    rows_x = propagator.shape[-2]
    cols_yz = propagator.shape[-1]
    rows_y = cols_yz // EXTENT
    site_count = rows_x * cols_yz
    grid_x = lax.axis_size("gx")
    grid_y = lax.axis_size("gy")
    cosine, sine_table = dft_tables(EXTENT)

    def one_slice(slice_block):
        flattened = slice_block.reshape(2, 4, 3, 4, 3, site_count)
        prod_real, prod_imag = spin_products(flattened[0], flattened[1])
        prod_stack = jnp.concatenate([prod_real, prod_imag], axis=0).astype(jnp.bfloat16)
        dens_real = jnp.dot(stack_real, prod_stack, preferred_element_type=jnp.float32).astype(
            jnp.bfloat16
        )
        dens_imag = jnp.dot(stack_imag, prod_stack, preferred_element_type=jnp.float32).astype(
            jnp.bfloat16
        )
        view = (dens_real.shape[0], rows_x * rows_y, EXTENT)
        dens_real = dens_real.reshape(view)
        dens_imag = dens_imag.reshape(view)

        def along(values, weights):
            return jnp.einsum("cpz,zk->ckp", values, weights, preferred_element_type=jnp.float32)

        new_real = along(dens_real, cosine) + along(dens_imag, sine_table)
        new_imag = along(dens_imag, cosine) - along(dens_real, sine_table)
        return (new_real.astype(jnp.bfloat16), new_imag.astype(jnp.bfloat16))

    along_z = lax.map(one_slice, propagator)

    def arrange(values):
        shape_in = values.shape
        values = values.reshape(
            shape_in[0], shape_in[1], shape_in[2], grid_x, grid_y, rows_x, rows_y
        )
        values = jnp.transpose(values, (0, 1, 2, 3, 5, 4, 6))
        return values.reshape(shape_in[0], shape_in[1], shape_in[2], EXTENT, EXTENT)

    arranged = (
        arrange(lax.all_to_all(along_z[0], ("gx", "gy"), split_axis=2, concat_axis=3, tiled=True)),
        arrange(lax.all_to_all(along_z[1], ("gx", "gy"), split_axis=2, concat_axis=3, tiled=True)),
    )
    arranged = transform(arranged, 4, jnp.bfloat16, cosine, sine_table)
    spec_real, spec_imag = transform(arranged, 3, jnp.float32, cosine, sine_table)
    return jnp.concatenate([spec_real, spec_imag], axis=4)


def solution(mesh):
    return jax.shard_map(
        body,
        mesh=mesh,
        in_specs=(P("ta", None, None, None, None, None, "gx", "gy"), P()),
        out_specs=P("ta", None, ("gx", "gy"), None, None),
        check_vma=False,
    )
```

profile of v0, /device:TPU:1, one launch (start us, length us, event | category | flops | bytes accessed | tf_op | source)
XLA Modules:
  0.0 207.8 jit_solution(4332045447886033136)
XLA Ops:
  0.0 0.7 convert_subtract_fusion.1
  0.7 4.4 %fusion.124 = (bf16[1,1,4,3,4,3,8,1024]{7,6,5,4,3,2,1,0:T(8,128)(2,1)S(1)}, bf16[1,1,4,3,4,3,8,1024]{7,6,5,4,3,2,1,0:T(8,128)(2,1)}) fusion(bf16[1,2,4,3,4,3,8,1024]{7,6,5,4,3,2,1,0:T(8,128)(2,1)} %param.2), kind=kLoop, calls=%fused_computation.175 | loop fusion | bytes 9437184 | tf_op jit(solution)/shard_map/while/body/eval_jaxpr/slice | solution.py:94
  5.1 1.6 copy.49
  6.7 5.1 %squeeze.47 = bf16[4,3,4,3,8192]{4,2,3,1,0:T(4,128)(2,1)S(1)} reshape(bf16[1,1,4,3,4,3,8,1024]{7,6,4,5,3,2,1,0:T(8,128)(2,1)} %copy.49) | data formatting | bytes 4718592 | tf_op jit(solution)/shard_map/while/body/eval_jaxpr/squeeze | solution.py:94
  11.8 3.4 %copy.50 = bf16[1,1,4,3,4,3,8,1024]{7,6,4,5,3,2,1,0:T(8,128)(2,1)} copy(bf16[1,1,4,3,4,3,8,1024]{7,6,5,4,3,2,1,0:T(8,128)(2,1)} %get-tuple-element.22) | data formatting | bytes 4718592 | tf_op jit(solution)/shard_map/while/body/eval_jaxpr/slice | solution.py:94
  15.2 6.2 %squeeze.48 = bf16[4,3,4,3,8192]{4,2,3,1,0:T(4,128)(2,1)} reshape(bf16[1,1,4,3,4,3,8,1024]{7,6,4,5,3,2,1,0:T(8,128)(2,1)} %copy.50) | data formatting | bytes 4718592 | tf_op jit(solution)/shard_map/while/body/eval_jaxpr/squeeze | solution.py:94
  21.3 2.5 %fusion.24 = (f32[4,4,8192]{2,1,0:T(4,128)S(1)}, f32[4,4,8192]{2,1,0:T(4,128)S(1)}, f32[4,4,8192]{2,1,0:T(4,128)S(1)}, f32[4,4,8192]{2,1,0:T(4,128)S(1)}, f32[4,...) fusion(bf16[4,3,4,3,8192]{4,2,3,1,0:T(4,128)(2,1)} %squeeze.48,, ...), kind=kLoop, calls=%fused_computation.59 | loop fusion | flops 2359296 | bytes 14155776 | tf_op jit(solution)/shard_map/while/body/eval_jaxpr/convert_element_type | solution.py:41
  23.9 37.5 %add_add_fusion = (f32[4,4,4,4,8192]{4,3,2,1,0:T(4,128)}, f32[4,4,4,4,8192]{4,3,2,1,0:T(4,128)}) fusion(f32[4,4,8192]{2,1,0:T(4,128)S(1)} %get-tuple-element.44, f32[4,4,8192]{2,1,0:T(4,128)S(1)} %get-tuple-element.70, f32[4,4,8192]{2,1,0:T(4,128)S(1)} %get-tuple-element.45, f32[4,4,8192]{2,1,0:T(4,128)S(1)} %get-tuple-element.69, ...), kind=kLoop, calls=%fused_computation.4 | loop fusion | flops 130023424 | bytes 25165824 | tf_op jit(solution)/shard_map/while/body/eval_jaxpr/add | solution.py:43
  61.4 10.0 %reshape.473 = f32[256,8192]{1,0:T(8,128)} reshape(f32[4,4,4,4,8192]{4,3,2,1,0:T(4,128)} %get-tuple-element.19) | data formatting | bytes 16777216 | tf_op jit(solution)/shard_map/while/body/eval_jaxpr/add | solution.py:43
  71.5 12.5 %broadcast_multiply_fusion.2 = (f32[4,4,4,4,8192]{4,3,2,1,0:T(4,128)}, f32[4,4,4,4,8192]{4,3,2,1,0:T(4,128)}, f32[4,4,4,4,8192]{4,3,2,1,0:T(4,128)}, f32[4,4,4,4,8192]{4,3,2,1,0:T(4,128)}) fusion(f32[4,4,8192]{2,1,0:T(4,128)S(1)} %get-tuple-element.43, f32[4,4,8192]{2,1,0:T(4,128)S(1)} %get-tuple-element.71), kind=kLoop, calls=%fused_computation.9 | loop fusion | flops 8388608 | bytes 34603008 | tf_op jit(solution)/shard_map/while/body/eval_jaxpr/mul | solution.py:49
  83.9 10.0 %mul.987 = f32[256,8192]{1,0:T(8,128)} reshape(f32[4,4,4,4,8192]{4,3,2,1,0:T(4,128)} %get-tuple-element.53) | data formatting | bytes 16777216 | tf_op jit(solution)/shard_map/while/body/eval_jaxpr/mul | solution.py:44
  93.9 10.0 %mul.991 = f32[256,8192]{1,0:T(8,128)} reshape(f32[4,4,4,4,8192]{4,3,2,1,0:T(4,128)} %get-tuple-element.54) | data formatting | bytes 16777216 | tf_op jit(solution)/shard_map/while/body/eval_jaxpr/mul | solution.py:45
  103.9 10.0 %reshape.474 = f32[256,8192]{1,0:T(8,128)} reshape(f32[4,4,4,4,8192]{4,3,2,1,0:T(4,128)} %get-tuple-element.20) | data formatting | bytes 16777216 | tf_op jit(solution)/shard_map/while/body/eval_jaxpr/sub | solution.py:48
  113.9 10.0 %mul.1021 = f32[256,8192]{1,0:T(8,128)} reshape(f32[4,4,4,4,8192]{4,3,2,1,0:T(4,128)} %get-tuple-element.51) | data formatting | bytes 16777216 | tf_op jit(solution)/shard_map/while/body/eval_jaxpr/mul | solution.py:49
  124.0 0.0 slice-start
  124.0 10.0 %mul.1023 = f32[256,8192]{1,0:T(8,128)} reshape(f32[4,4,4,4,8192]{4,3,2,1,0:T(4,128)} %get-tuple-element.52) | data formatting | bytes 16777216 | tf_op jit(solution)/shard_map/while/body/eval_jaxpr/mul | solution.py:50
  134.0 0.0 slice-done
  134.0 0.1 fusion.28
  134.1 0.1 copy.47
  134.2 0.1 copy.48
  134.3 0.0 copy-start
  134.3 0.0 copy-start.1
  134.3 9.1 %add_convert_fusion = bf16[256,8192]{1,0:T(8,128)(2,1)S(1)} fusion(f32[256,8192]{1,0:T(8,128)} %mul.991, f32[256,8192]{1,0:T(8,128)} %reshape.473, f32[256,8192]{1,0:T(8,128)} %mul.987), kind=kLoop, calls=%fused_computation.6 | loop fusion | flops 6291456 | bytes 29360128 | tf_op jit(solution)/shard_map/convert.20
  143.4 1.5 copy-done
  144.9 2.4 %copy-done.1 = f32[256,8192]{1,0:T(8,128)S(1)} copy-done((f32[256,8192]{1,0:T(8,128)S(1)}, f32[256,8192]{1,0:T(8,128)}, u32[]{:S(2)}) %copy-start.1) | copy-done | bytes 8388632
  147.3 0.0 copy-start.2
  147.3 7.1 %subtract_convert_fusion = bf16[256,8192]{1,0:T(8,128)(2,1)} fusion(f32[256,8192]{1,0:T(8,128)S(1)} %copy-done.1, f32[256,8192]{1,0:T(8,128)} %reshape.474, f32[256,8192]{1,0:T(8,128)S(1)} %copy-done), kind=kLoop, calls=%fused_computation.5 | loop fusion | flops 6291456 | bytes 29360128 | tf_op jit(solution)/shard_map/convert.21
  154.4 0.0 copy-done.2
  154.4 4.0 %convolution_convert_fusion.1 = bf16[16,8192]{1,0:T(8,128)(2,1)S(1)} fusion(bf16[256,8192]{1,0:T(8,128)(2,1)} %subtract_convert_fusion, bf16[256,8192]{1,0:T(8,128)(2,1)S(1)} %add_convert_fusion, bf16[16,256]{1,0:T(8,128)(2,1)S(1)} %copy.48, bf16[16,256]{1,0:T(8,128)(2,1)S(1)} %copy.47), kind=kOutput, calls=%fused_computation.1 | convolution fusion | flops 151158784 | bytes 8667136 | tf_op jit(solution)/shard_map/while/body/eval_jaxpr/dot_general | solution.py:96
  158.4 0.5 reshape.423
  159.0 0.4 fusion.58
  159.3 0.1 copy.52
  159.4 4.7 %convolution_convert_fusion = bf16[16,8192]{1,0:T(8,128)(2,1)S(1)} fusion(bf16[256,8192]{1,0:T(8,128)(2,1)} %subtract_convert_fusion, bf16[256,8192]{1,0:T(8,128)(2,1)} %copy-done.2, bf16[16,256]{1,0:T(8,128)(2,1)S(1)} %copy.47, bf16[16,256]{1,0:T(8,128)(2,1)S(1)} %copy.52), kind=kOutput, calls=%fused_computation | convolution fusion | flops 151158784 | bytes 8667136 | tf_op jit(solution)/shard_map/while/body/eval_jaxpr/dot_general | solution.py:99
  164.1 0.5 reshape.424
  164.7 0.4 fusion.7
  165.0 0.9 copy.55
  165.9 7.1 %all-to-all-start = ((bf16[1,16,64,128]{3,1,0,2:T(8,128)(2,1)}), bf16[1,16,64,128]{3,1,0,2:T(8,128)(2,1)S(1)}, u32[]{:S(2)}, u32[]{:S(2)}) async-start(bf16[1,16,64,128]{3,1,0,2:T(8,128)(2,1)} %copy.55), calls=%async_computation | async-start | bytes 524288 | tf_op jit(solution)/shard_map/all_to_all | solution.py:124
  173.0 0.4 fusion.56
  173.4 0.4 fusion.6
  173.8 0.9 copy.61
  174.7 8.7 %all-to-all-done = bf16[1,16,64,128]{3,1,0,2:T(8,128)(2,1)S(1)} async-done(((bf16[1,16,64,128]{3,1,0,2:T(8,128)(2,1)}), bf16[1,16,64,128]{3,1,0,2:T(8,128)(2,1)S(1)}, u32[]{:S(2)}, u32[]{:S(2)}) %all-to-all-start) | async-done | bytes 262176 | tf_op jit(solution)/shard_map/all_to_all | solution.py:124
  183.3 2.6 %all-to-all-start.1 = ((bf16[1,16,64,128]{3,1,0,2:T(8,128)(2,1)}), bf16[1,16,64,128]{3,1,0,2:T(8,128)(2,1)S(1)}, u32[]{:S(2)}, u32[]{:S(2)}) async-start(bf16[1,16,64,128]{3,1,0,2:T(8,128)(2,1)} %copy.61), calls=%async_computation.1 | async-start | bytes 524288 | tf_op jit(solution)/shard_map/all_to_all | solution.py:125
  185.9 0.1 copy.84
  186.0 2.3 %reshape.425 = bf16[1,16,2,8,4,8,16]{6,5,4,3,2,1,0:T(8,128)(2,1)} reshape(bf16[1,16,2,32,128]{4,3,2,1,0:T(8,128)(2,1)S(1)} %bitcast.181) | data formatting | bytes 524288 | tf_op jit(solution)/shard_map/reshape | solution.py:117
  188.4 2.7 %copy.57 = bf16[1,16,2,8,8,4,16]{6,5,4,3,2,1,0:T(4,128)(2,1)S(1)} copy(bf16[1,16,2,8,8,4,16]{6,4,5,3,2,1,0:T(8,128)(2,1)} %bitcast.179) | data formatting | bytes 524288 | tf_op jit(solution)/shard_map/transpose | solution.py:120
  191.0 1.1 reshape.426
  192.1 1.4 fusion.52
  193.5 2.7 %all-to-all-done.1 = bf16[1,16,64,128]{3,1,0,2:T(8,128)(2,1)S(1)} async-done(((bf16[1,16,64,128]{3,1,0,2:T(8,128)(2,1)}), bf16[1,16,64,128]{3,1,0,2:T(8,128)(2,1)S(1)}, u32[]{:S(2)}, u32[]{:S(2)}) %all-to-all-start.1) | async-done | bytes 262176 | tf_op jit(solution)/shard_map/all_to_all | solution.py:125
  196.2 0.1 copy.83
  196.3 2.3 %reshape.427 = bf16[1,16,2,8,4,8,16]{6,5,4,3,2,1,0:T(8,128)(2,1)} reshape(bf16[1,16,2,32,128]{4,3,2,1,0:T(8,128)(2,1)S(1)} %bitcast.182) | data formatting | bytes 524288 | tf_op jit(solution)/shard_map/reshape | solution.py:117
  198.7 2.7 %copy.63 = bf16[1,16,2,8,8,4,16]{6,5,4,3,2,1,0:T(4,128)(2,1)S(1)} copy(bf16[1,16,2,8,8,4,16]{6,4,5,3,2,1,0:T(8,128)(2,1)} %bitcast.180) | data formatting | bytes 524288 | tf_op jit(solution)/shard_map/transpose | solution.py:120
  201.3 1.1 reshape.428
  202.4 0.4 fusion.46
  202.8 1.6 fusion.2
  204.5 0.4 fusion.48
  204.9 0.4 fusion.3
  205.3 0.4 fusion.50
  205.7 0.4 fusion.1
  206.1 0.4 fusion
  206.5 1.3 pad_maximum_fusion.3
  (2 shorter events, 0.0 us)
Async XLA Ops:
  124.0 10.1 %slice-start = ((s32[16,8]{0,1:T(8,128)}), s32[16,4]{0,1:T(4,128)S(1)}, s32[]{:S(2)}) async-start(s32[16,8]{0,1:T(8,128)} %param.3), calls=%async_computation.2 | async-start | bytes 4096 | tf_op jit(solution)/shard_map/slice | solution.py:13
  134.3 10.6 %copy-start = (f32[256,8192]{1,0:T(8,128)S(1)}, f32[256,8192]{1,0:T(8,128)}, u32[]{:S(2)}) copy-start(f32[256,8192]{1,0:T(8,128)} %mul.1021) | copy-start | bytes 25165828
  134.3 13.0 %copy-start.1 = (f32[256,8192]{1,0:T(8,128)S(1)}, f32[256,8192]{1,0:T(8,128)}, u32[]{:S(2)}) copy-start(f32[256,8192]{1,0:T(8,128)} %mul.1023) | copy-start | bytes 25165828
  147.3 7.1 %copy-start.2 = (bf16[256,8192]{1,0:T(8,128)(2,1)}, bf16[256,8192]{1,0:T(8,128)(2,1)S(1)}, u32[]{:S(2)}) copy-start(bf16[256,8192]{1,0:T(8,128)(2,1)S(1)} %add_convert_fusion) | copy-start | bytes 12582916
  165.9 17.4 %all-to-all-start = ((bf16[1,16,64,128]{3,1,0,2:T(8,128)(2,1)}), bf16[1,16,64,128]{3,1,0,2:T(8,128)(2,1)S(1)}, u32[]{:S(2)}, u32[]{:S(2)}) async-start(bf16[1,16,64,128]{3,1,0,2:T(8,128)(2,1)} %copy.55), calls=%async_computation | async-start | bytes 524288 | tf_op jit(solution)/shard_map/all_to_all | solution.py:124
  183.3 12.9 %all-to-all-start.1 = ((bf16[1,16,64,128]{3,1,0,2:T(8,128)(2,1)}), bf16[1,16,64,128]{3,1,0,2:T(8,128)(2,1)S(1)}, u32[]{:S(2)}, u32[]{:S(2)}) async-start(bf16[1,16,64,128]{3,1,0,2:T(8,128)(2,1)} %copy.61), calls=%async_computation.1 | async-start | bytes 524288 | tf_op jit(solution)/shard_map/all_to_all | solution.py:125
where the time goes:
time: 210 us; the launch traced here: 208 us
  local copies, waits for them, and re-layouts  100 us (48%)
  other arithmetic  70.8 us (34%)
  matrix products  15.7 us (7%)
  waiting for transfers between devices  11.4 us (5%)
  starting transfers between devices  9.66 us (5%)
    add x1, other arithmetic, spin_products(): total_real + left_real[:, :, None, None] * left_real[None, None]  37.5 us
    another operation x3, other arithmetic  16.3 us
    mul x1, other arithmetic, spin_products(): left_imag[:, :, None, None] * left_real[None, None]  12.5 us
    squeeze x2, local copies, waits for them, and re-layouts, one_slice(): prod_real, prod_imag = spin_products(flattened[0], flattened[1])  11.3 us
    mul x1, local copies, waits for them, and re-layouts, spin_products(): left_real[:, :, None, None] * left_imag[None, None]  10 us
    add x1, local copies, waits for them, and re-layouts, spin_products(): total_real + left_real[:, :, None, None] * left_real[None, None]  10 us
    mul x1, local copies, waits for them, and re-layouts, spin_products(): left_imag[:, :, None, None] * left_real[None, None]  10 us
    mul x1, local copies, waits for them, and re-layouts, spin_products(): left_imag[:, :, None, None] * left_imag[None, None]  10 us
  transfers between devices with their start and end apart: 2, of which 2 were waited for; matrix products, arithmetic and copies ran while one was open for 4% of the time, Pallas kernels for 0%

commit v1 on v0

v1 whole, which is shorter than its diff:
```python
import functools
import math

import jax
import jax.numpy as jnp
import numpy as np
from jax import lax
from jax.experimental import pallas as pl
from jax.experimental.pallas import tpu as pltpu
from jax.sharding import PartitionSpec as P

LANES = 128
SPINS = 4
PAIRS = SPINS * SPINS
SLOTS = PAIRS * PAIRS


def dft_tables(length):
    index = np.arange(length)
    angles = (index[:, None] * index[None, :] % length) * (2.0 * math.pi / length)
    norm = 1.0 / math.sqrt(length)
    return np.cos(angles) * norm, np.sin(angles) * norm


def z_matrix(length, lane_rows, per_device):
    cosine, sine = dft_tables(length)
    mix = np.array([[cosine, sine], [-sine, cosine]])
    eye = np.eye(lane_rows)
    full = np.einsum("oizk,yv->koyivz", mix, eye)
    return full.reshape(length * 2 * lane_rows, 2 * lane_rows * length)


def y_matrix(length, grid_y, steps, lane_rows, per_device):
    cosine, sine = dft_tables(length)
    cosine = cosine.reshape(grid_y, steps, lane_rows, length)
    sine = sine.reshape(grid_y, steps, lane_rows, length)
    real = np.stack([cosine, sine])
    imag = np.stack([-sine, cosine])
    plain = np.stack([real, imag])
    turned = np.stack([imag, -real])
    both = np.stack([plain, turned])
    full = np.einsum("aoigjvk,pq->gjpivaqok", both, np.eye(per_device))
    rows = grid_y * steps * per_device * 2 * lane_rows
    return full.reshape(rows, 2 * per_device * 2 * length)


def density_weights(table):
    count = table.shape[0]
    slot = lax.broadcasted_iota(jnp.int32, (count, SLOTS), 1)
    s1, s2, s3, s4 = (slot >> 6) & 3, (slot >> 4) & 3, (slot >> 2) & 3, slot & 3

    def pick(spin, base):
        value = jnp.broadcast_to(table[:, base : base + 1], (count, SLOTS))
        for q in range(1, SPINS):
            other = jnp.broadcast_to(table[:, base + q : base + q + 1], (count, SLOTS))
            value = jnp.where(spin == q, other, value)
        return value

    def weight(a1, a2, b1, b2):
        hit = (a1 == pick(b1, 0)) & (b2 == pick(a2, 0))
        code = (pick(b1, SPINS) + pick(a2, SPINS)) & 3
        real = jnp.where(code == 0, 1.0, 0.0) - jnp.where(code == 2, 1.0, 0.0)
        imag = jnp.where(code == 1, 1.0, 0.0) - jnp.where(code == 3, 1.0, 0.0)
        return jnp.where(hit, real, 0.0), jnp.where(hit, imag, 0.0)

    here_r, here_i = weight(s1, s2, s3, s4)
    swap_r, swap_i = weight(s3, s4, s1, s2)
    first, second = slot >> 4, slot & 15
    upper, diagonal = first < second, first == second
    real = jnp.where(diagonal, here_r, jnp.where(upper, here_r + swap_r, here_i - swap_i))
    imag = jnp.where(diagonal, here_i, jnp.where(upper, here_i + swap_i, swap_r - here_r))
    return jnp.concatenate([real, imag], axis=0)


def front_kernel(prop, table, zmat, out, weights, gram, *, tiles, colors, rows_x, owners):
    @pl.when((pl.program_id(0) == 0) & (pl.program_id(1) == 0))
    def _():
        weights[...] = density_weights(table[...]).astype(jnp.bfloat16)

    channels = weights.shape[0] // 2
    pieces = []
    for tile in range(tiles):
        lanes = pl.ds(tile * LANES, LANES)

        def site(part, pair, tile_lanes=lanes):
            s1, s2 = divmod(pair, SPINS)
            return [
                prop[0, part, s1, c1, s2, c2, :, tile_lanes].astype(jnp.float32)
                for c1 in range(colors)
                for c2 in range(colors)
            ]

        def put(a, b, value, tile=tile):
            gram[tile, pl.ds((a * PAIRS + b) * rows_x, rows_x), :] = value

        def total(left, right):
            acc = left[0] * right[0]
            for x, y in zip(left[1:], right[1:]):
                acc = acc + x * y
            return acc

        for a in range(PAIRS):
            ar, ai = site(0, a), site(1, a)
            asum = [x + y for x, y in zip(ar, ai)]
            put(a, a, total(ar, ar) + total(ai, ai))
            for b in range(a + 1, PAIRS):
                br, bi = site(0, b), site(1, b)
                p, q = total(ar, br), total(ai, bi)
                t = total(asum, [x - y for x, y in zip(br, bi)])
                put(a, b, p + q)
                put(b, a, (t - p) + q)
        for x in range(rows_x):
            products = gram[tile, pl.ds(x, SLOTS, stride=rows_x), :].astype(jnp.bfloat16)
            dens = jnp.dot(weights[...], products, preferred_element_type=jnp.float32)
            dens = dens.astype(jnp.bfloat16)
            pieces.append(jnp.concatenate([dens[:channels], dens[channels:]], axis=1))
    stacked = jnp.concatenate(pieces, axis=0)
    turned = lax.dot_general(
        zmat[...], stacked, (((1,), (1,)), ((), ())), preferred_element_type=jnp.float32
    )
    width = rows_x * channels
    rows = turned.shape[0] // owners
    turned = turned.reshape(owners, rows, tiles * width)
    out[0] = jnp.concatenate(
        [turned[:, :, k * width : (k + 1) * width] for k in range(tiles)], axis=1
    ).astype(jnp.bfloat16)


def back_kernel(data, ymat, xmat, out, lined, *, grid_x, rows_x, channels, pitch, per_device):
    cols = ymat.shape[1]
    blocks = cols // LANES
    for gx in range(grid_x):
        turned = lax.dot_general(
            data[0, gx], ymat[...], (((0,), (0,)), ((), ())), preferred_element_type=jnp.float32
        )
        for block in range(blocks):
            for x in range(rows_x):
                lined[block, gx, pl.ds(x * pitch, channels), :] = turned[
                    x * channels : (x + 1) * channels, block * LANES : (block + 1) * LANES
                ]
    for c in range(channels):
        sides = []
        for block in range(blocks):
            lines = [
                lined[block, gx, pl.ds(c, rows_x, stride=pitch), :] for gx in range(grid_x)
            ]
            sides.append(jnp.concatenate(lines, axis=0).astype(jnp.bfloat16))
        half = blocks // 2
        right = jnp.concatenate(
            [jnp.concatenate(sides[:half], axis=1), jnp.concatenate(sides[half:], axis=1)], axis=0
        )
        spectrum = jnp.dot(xmat[...], right, preferred_element_type=jnp.float32)
        width = cols // 2 // per_device
        for k in range(per_device):
            out[0, c, k] = spectrum[:, k * width : (k + 1) * width]


def body(propagator, gamma_table):
    slices, _, _, colors, _, _, rows_x, cols_yz = propagator.shape
    channels = gamma_table.shape[0]
    grid_x, grid_y = lax.axis_size("gx"), lax.axis_size("gy")
    owners = grid_x * grid_y
    extent = rows_x * grid_x
    per_device = extent // owners
    lane_rows = LANES // extent
    steps = cols_yz // LANES
    tiles = 2
    zmat = jnp.asarray(z_matrix(extent, lane_rows, per_device), jnp.bfloat16)
    ymat = jnp.asarray(y_matrix(extent, grid_y, steps, lane_rows, per_device), jnp.bfloat16)
    cosine, sine = dft_tables(extent)
    xmat = jnp.asarray(np.concatenate([cosine.T, sine.T], axis=1), jnp.bfloat16)

    width = rows_x * channels
    rows = steps * per_device * 2 * lane_rows
    step_rows = tiles * per_device * 2 * lane_rows
    sent = pl.pallas_call(
        functools.partial(
            front_kernel, tiles=tiles, colors=colors, rows_x=rows_x, owners=owners
        ),
        grid=(slices, steps // tiles),
        in_specs=[
            pl.BlockSpec(
                (1, 2, SPINS, colors, SPINS, colors, rows_x, tiles * LANES),
                lambda t, j: (t, 0, 0, 0, 0, 0, 0, j),
            ),
            pl.BlockSpec(gamma_table.shape, lambda t, j: (0, 0)),
            pl.BlockSpec(zmat.shape, lambda t, j: (0, 0)),
        ],
        out_specs=pl.BlockSpec((1, owners, step_rows, width), lambda t, j: (t, 0, j, 0)),
        out_shape=jax.ShapeDtypeStruct((slices, owners, rows, width), jnp.bfloat16),
        scratch_shapes=[
            pltpu.VMEM((2 * channels, SLOTS), jnp.bfloat16),
            pltpu.VMEM((tiles, SLOTS * rows_x, LANES), jnp.float32),
        ],
        name="front",
    )(propagator, gamma_table, zmat)

    got = lax.all_to_all(sent, ("gx", "gy"), split_axis=1, concat_axis=1, tiled=True)
    got = got.reshape(slices, grid_x, grid_y * rows, width)

    pitch = channels + 8
    return pl.pallas_call(
        functools.partial(
            back_kernel,
            grid_x=grid_x,
            rows_x=rows_x,
            channels=channels,
            pitch=pitch,
            per_device=per_device,
        ),
        grid=(slices,),
        in_specs=[
            pl.BlockSpec((1, grid_x, grid_y * rows, width), lambda t: (t, 0, 0, 0)),
            pl.BlockSpec(ymat.shape, lambda t: (0, 0)),
            pl.BlockSpec(xmat.shape, lambda t: (0, 0)),
        ],
        out_specs=pl.BlockSpec(
            (1, channels, per_device, extent, 2 * extent), lambda t: (t, 0, 0, 0, 0)
        ),
        out_shape=jax.ShapeDtypeStruct(
            (slices, channels, per_device, extent, 2 * extent), jnp.float32
        ),
        scratch_shapes=[
            pltpu.VMEM((ymat.shape[1] // LANES, grid_x, rows_x * pitch, LANES), jnp.float32)
        ],
        name="back",
    )(got, ymat, xmat)


def solution(mesh):
    return jax.shard_map(
        body,
        mesh=mesh,
        in_specs=(P("ta", None, None, None, None, None, "gx", "gy"), P()),
        out_specs=P("ta", None, ("gx", "gy"), None, None),
        check_vma=False,
    )
```

time: 210 us -> 43.9 us (0.21)
  local copies, waits for them, and re-layouts: 100 us -> 1.35 us
  other arithmetic: 70.8 us -> 0 us
  blocking collectives: 0 us -> 22.5 us
  Pallas kernels: 0 us -> 19.8 us
  matrix products: 15.7 us -> 0 us
  waiting for transfers between devices: 11.4 us -> 0 us
  starting transfers between devices: 9.66 us -> 0 us
    mul x4 -> x0, local copies, waits for them, and re-layouts: 40.1 us -> none  [the longest x1 10 us: spin_products(): left_real[:, :, None, None] * left_imag[None, None]]
    add x2 -> x0, other arithmetic: 37.6 us -> none  [the longest x1 37.5 us: spin_products(): total_real + left_real[:, :, None, None] * left_real[None, None]]
    all_to_all x0 -> x1, blocking collectives: none -> 22.5 us  [body(): lax.all_to_all(sent, ('gx', 'gy'), split_axis=1, concat_axis=1, tiled=True)]
    pallas_call x0 -> x2, Pallas kernels: none -> 19.8 us  [the longest x1 16.8 us: body(): pl.pallas_call(functools.partial(front_kernel, tiles=tiles, colors=colors...]
    another operation x3 -> x0, other arithmetic: 16.3 us -> none
    dot_general x14 -> x0, matrix products: 15.7 us -> none  [the longest x8 5.45 us: contract_axis(): jnp.tensordot(values, weights, axes=([which_axis], [0]), preferred_elemen...]
    mul x1 -> x0, other arithmetic: 12.5 us -> none  [spin_products(): left_imag[:, :, None, None] * left_real[None, None]]
    all_to_all x2 -> x0, waiting for transfers between devices: 11.4 us -> none  [the longest x1 8.66 us: body(): lax.all_to_all(along_z[0], ('gx', 'gy'), split_axis=2, concat_axis=3, til...]
  transfers between devices with their start and end apart: 2 -> 0, of which waited for: 2 -> 0; matrix products, arithmetic and copies ran while one was open for 4% -> 0% of each run, Pallas kernels for 0% -> 0%
where the time goes in v1:
time: 43.9 us; the launch traced here: 43.7 us
  blocking collectives  22.5 us (51%)
  Pallas kernels  19.8 us (45%)
  local copies, waits for them, and re-layouts  1.35 us (3%)
    all_to_all x1, blocking collectives, body(): lax.all_to_all(sent, ('gx', 'gy'), split_axis=1, concat_axis=1, tiled=True)  22.5 us
    pallas_call x1, Pallas kernels, body(): pl.pallas_call(functools.partial(front_kernel, tiles=tiles, colors=colors...  16.8 us
    pallas_call x1, Pallas kernels, body(): pl.pallas_call(functools.partial(back_kernel, grid_x=grid_x, rows_x=rows_...  3.03 us
    unnamed x1, local copies, waits for them, and re-layouts  1.35 us

profile of v1, /device:TPU:1, one launch (start us, length us, event | category | flops | bytes accessed | tf_op | source)
XLA Modules:
  0.0 43.7 jit_solution(15301936675211933660)
XLA Ops:
  0.0 1.4 %copy.7.table = s32[16,8]{1,0:T(8,128)} copy(s32[16,8]{0,1:T(8,128)} %param.6) | data formatting | bytes 1024 | tf_op args[1]
  1.4 16.8 %front.1 = bf16[1,32,64,128]{3,2,1,0:T(8,128)(2,1)} custom-call(bf16[1,2,4,3,4,3,8,1024]{7,6,5,4,3,2,1,0:T(8,128)(2,1)} %prop.1, s32[16,8]{1,0:T(8,128)} %copy.7.table, bf16[256,256]{1,0:T(8,128)(2,1)} %constant.6.clone.zmat), custom_call_target="tpu_custom_call" | custom-call | tf_op jit(solution)/shard_map/front/pallas_call | solution.py:176
  18.2 22.5 %all_to_all.5 = bf16[1,32,64,128]{3,2,0,1:T(8,128)(2,1)} all-to-all(bf16[1,32,64,128]{3,2,0,1:T(8,128)(2,1)} %bitcast.3), channel_id=1, replica_groups=mesh['ta'=1,'gx'=8,'gy'=4] {'gx','gy'}, dimensions={1} | all-to-all | bytes 1048576 | tf_op jit(solution)/shard_map/all_to_all | solution.py:198
  40.6 3.0 %back.1 = f32[1,16,2,64,128]{4,3,2,1,0:T(8,128)} custom-call(bf16[1,8,256,128]{3,2,1,0:T(8,128)(2,1)} %bitcast.2, bf16[256,512]{1,0:T(8,128)(2,1)} %constant.7.clone.ymat, bf16[64,128]{1,0:T(8,128)(2,1)} %constant.8.clone.xmat), custom_call_target="tpu_custom_call" | custom-call | tf_op jit(solution)/shard_map/back/pallas_call | solution.py:202

commit v2 on v1

--- a/solution.py
+++ b/solution.py
@@ -47,7 +47,10 @@
 def density_weights(table):
     count = table.shape[0]
     slot = lax.broadcasted_iota(jnp.int32, (count, SLOTS), 1)
-    s1, s2, s3, s4 = (slot >> 6) & 3, (slot >> 4) & 3, (slot >> 2) & 3, slot & 3
+    first, step = slot >> 4, slot & 15
+    is_real = (step < 8) | ((step == 8) & (first < 8))
+    second = (first + jnp.where(step > 8, step - 8, step)) & 15
+    s1, s2, s3, s4 = first >> 2, first & 3, second >> 2, second & 3
 
     def pick(spin, base):
         value = jnp.broadcast_to(table[:, base : base + 1], (count, SLOTS))
@@ -65,33 +68,35 @@
 
     here_r, here_i = weight(s1, s2, s3, s4)
     swap_r, swap_i = weight(s3, s4, s1, s2)
-    first, second = slot >> 4, slot & 15
-    upper, diagonal = first < second, first == second
-    real = jnp.where(diagonal, here_r, jnp.where(upper, here_r + swap_r, here_i - swap_i))
-    imag = jnp.where(diagonal, here_i, jnp.where(upper, here_i + swap_i, swap_r - here_r))
+    single = step == 0
+    real = jnp.where(single, here_r, jnp.where(is_real, here_r + swap_r, swap_i - here_i))
+    imag = jnp.where(single, here_i, jnp.where(is_real, here_i + swap_i, here_r - swap_r))
     return jnp.concatenate([real, imag], axis=0)
 
 
-def front_kernel(prop, table, zmat, out, weights, gram, *, tiles, colors, rows_x, owners):
+def front_kernel(prop, table, zmat, out, weights, packed, gram, *, tiles, colors, rows_x, owners):
     @pl.when((pl.program_id(0) == 0) & (pl.program_id(1) == 0))
     def _():
-        weights[...] = density_weights(table[...]).astype(jnp.bfloat16)
+        weights[...] = density_weights(jnp.transpose(table[...])).astype(jnp.bfloat16)
 
     channels = weights.shape[0] // 2
-    pieces = []
-    for tile in range(tiles):
-        lanes = pl.ds(tile * LANES, LANES)
-
-        def site(part, pair, tile_lanes=lanes):
-            s1, s2 = divmod(pair, SPINS)
-            return [
-                prop[0, part, s1, c1, s2, c2, :, tile_lanes].astype(jnp.float32)
-                for c1 in range(colors)
-                for c2 in range(colors)
-            ]
-
-        def put(a, b, value, tile=tile):
-            gram[tile, pl.ds((a * PAIRS + b) * rows_x, rows_x), :] = value
+    spread = colors * colors
+    for pair in range(PAIRS):
+        s1, s2 = divmod(pair, SPINS)
+        for color in range(spread):
+            c1, c2 = divmod(color, colors)
+            for part in range(2):
+                wide = prop[0, part, s1, c1, s2, c2, :, :].astype(jnp.float32)
+                both = jnp.concatenate(
+                    [wide[:, k * LANES : (k + 1) * LANES] for k in range(tiles)], axis=0
+                )
+                packed[part, pair, color] = both.astype(jnp.bfloat16)
+                if part == 0:
+                    packed[2, pair, color] = (-both).astype(jnp.bfloat16)
+
+    def row(a, carry):
+        def load(part, pair):
+            return [packed[part, pair, color].astype(jnp.float32) for color in range(spread)]
 
         def total(left, right):
             acc = left[0] * right[0]
@@ -99,16 +104,28 @@
                 acc = acc + x * y
             return acc
 
-        for a in range(PAIRS):
-            ar, ai = site(0, a), site(1, a)
-            asum = [x + y for x, y in zip(ar, ai)]
-            put(a, a, total(ar, ar) + total(ai, ai))
-            for b in range(a + 1, PAIRS):
-                br, bi = site(0, b), site(1, b)
-                p, q = total(ar, br), total(ai, bi)
-                t = total(asum, [x - y for x, y in zip(br, bi)])
-                put(a, b, p + q)
-                put(b, a, (t - p) + q)
+        def put(d, value):
+            start = pl.multiple_of((a * PAIRS + d) * rows_x, rows_x)
+            for tile in range(tiles):
+                gram[tile, pl.ds(start, rows_x), :] = value[tile * rows_x : (tile + 1) * rows_x]
+
+        ar, ai, an = load(0, a), load(1, a), load(2, a)
+        put(0, total(ar + ai, ar + ai))
+        for d in range(1, PAIRS // 2 + 1):
+            b = (a + d) & (PAIRS - 1)
+            br, bi = load(0, b), load(1, b)
+            real, imag = total(ar + ai, br + bi), total(ai + an, br + bi)
+            if d < PAIRS // 2:
+                put(d, real)
+                put(d + PAIRS // 2, imag)
+            else:
+                put(d, jnp.where(a < PAIRS // 2, real, imag))
+        return carry
+
+    lax.fori_loop(0, PAIRS, row, 0)
+
+    pieces = []
+    for tile in range(tiles):
         for x in range(rows_x):
             products = gram[tile, pl.ds(x, SLOTS, stride=rows_x), :].astype(jnp.bfloat16)
             dens = jnp.dot(weights[...], products, preferred_element_type=jnp.float32)
@@ -183,17 +200,18 @@
                 (1, 2, SPINS, colors, SPINS, colors, rows_x, tiles * LANES),
                 lambda t, j: (t, 0, 0, 0, 0, 0, 0, j),
             ),
-            pl.BlockSpec(gamma_table.shape, lambda t, j: (0, 0)),
+            pl.BlockSpec(gamma_table.shape[::-1], lambda t, j: (0, 0)),
             pl.BlockSpec(zmat.shape, lambda t, j: (0, 0)),
         ],
         out_specs=pl.BlockSpec((1, owners, step_rows, width), lambda t, j: (t, 0, j, 0)),
         out_shape=jax.ShapeDtypeStruct((slices, owners, rows, width), jnp.bfloat16),
         scratch_shapes=[
             pltpu.VMEM((2 * channels, SLOTS), jnp.bfloat16),
+            pltpu.VMEM((3, PAIRS, colors * colors, tiles * rows_x, LANES), jnp.bfloat16),
             pltpu.VMEM((tiles, SLOTS * rows_x, LANES), jnp.float32),
         ],
         name="front",
-    )(propagator, gamma_table, zmat)
+    )(propagator, gamma_table.T, zmat)
 
     got = lax.all_to_all(sent, ("gx", "gy"), split_axis=1, concat_axis=1, tiled=True)
     got = got.reshape(slices, grid_x, grid_y * rows, width)

time: 43.9 us -> 36.2 us (0.82)
  Pallas kernels: 19.8 us -> 13.5 us
  local copies, waits for them, and re-layouts: 1.35 us -> 0 us
    pallas_call x1, Pallas kernels: 16.8 us -> 10.4 us  [body(): pl.pallas_call(functools.partial(front_kernel, tiles=tiles, colors=colors...]
    unnamed x1 -> x0, local copies, waits for them, and re-layouts: 1.35 us -> none
where the time goes in v2:
time: 36.2 us; the launch traced here: 35.9 us
  blocking collectives  22.5 us (62%)
  Pallas kernels  13.5 us (37%)
    all_to_all x1, blocking collectives, body(): lax.all_to_all(sent, ('gx', 'gy'), split_axis=1, concat_axis=1, tiled=True)  22.5 us
    pallas_call x1, Pallas kernels, body(): pl.pallas_call(functools.partial(front_kernel, tiles=tiles, colors=colors...  10.4 us
    pallas_call x1, Pallas kernels, body(): pl.pallas_call(functools.partial(back_kernel, grid_x=grid_x, rows_x=rows_...  3.03 us

profile of v2, /device:TPU:1, one launch (start us, length us, event | category | flops | bytes accessed | tf_op | source)
XLA Modules:
  0.0 35.9 jit_solution(9534266865607221395)
XLA Ops:
  0.0 10.4 %front.1 = bf16[1,32,64,128]{3,2,1,0:T(8,128)(2,1)} custom-call(bf16[1,2,4,3,4,3,8,1024]{7,6,5,4,3,2,1,0:T(8,128)(2,1)} %prop.1, s32[8,16]{1,0:T(8,128)} %bitcast.5, bf16[256,256]{1,0:T(8,128)(2,1)} %constant.6.clone.zmat), custom_call_target="tpu_custom_call" | custom-call | tf_op jit(solution)/shard_map/front/pallas_call | solution.py:193
  10.5 22.5 %all_to_all.5 = bf16[1,32,64,128]{3,2,0,1:T(8,128)(2,1)} all-to-all(bf16[1,32,64,128]{3,2,0,1:T(8,128)(2,1)} %bitcast.4), channel_id=1, replica_groups=mesh['ta'=1,'gx'=8,'gy'=4] {'gx','gy'}, dimensions={1} | all-to-all | bytes 1048576 | tf_op jit(solution)/shard_map/all_to_all | solution.py:216
  32.9 3.0 %back.1 = f32[1,16,2,64,128]{4,3,2,1,0:T(8,128)} custom-call(bf16[1,8,256,128]{3,2,1,0:T(8,128)(2,1)} %bitcast.3, bf16[256,512]{1,0:T(8,128)(2,1)} %constant.7.clone.ymat, bf16[64,128]{1,0:T(8,128)(2,1)} %constant.8.clone.xmat), custom_call_target="tpu_custom_call" | custom-call | tf_op jit(solution)/shard_map/back/pallas_call | solution.py:220

commit v3 on v2

--- a/solution.py
+++ b/solution.py
@@ -74,29 +74,28 @@
     return jnp.concatenate([real, imag], axis=0)
 
 
-def front_kernel(prop, table, zmat, out, weights, packed, gram, *, tiles, colors, rows_x, owners):
+def front_kernel(prop, table, zmat, out, weights, turned, gram, *, tiles, colors, rows_x, owners):
     @pl.when((pl.program_id(0) == 0) & (pl.program_id(1) == 0))
     def _():
         weights[...] = density_weights(jnp.transpose(table[...])).astype(jnp.bfloat16)
 
     channels = weights.shape[0] // 2
     spread = colors * colors
+
+    def narrow(part, s1, s2, color):
+        c1, c2 = divmod(color, colors)
+        wide = prop[0, part, s1, c1, s2, c2, :, :].astype(jnp.float32)
+        halves = [wide[:, k * LANES : (k + 1) * LANES] for k in range(tiles)]
+        return jnp.concatenate(halves, axis=0).astype(jnp.bfloat16)
+
     for pair in range(PAIRS):
-        s1, s2 = divmod(pair, SPINS)
         for color in range(spread):
-            c1, c2 = divmod(color, colors)
-            for part in range(2):
-                wide = prop[0, part, s1, c1, s2, c2, :, :].astype(jnp.float32)
-                both = jnp.concatenate(
-                    [wide[:, k * LANES : (k + 1) * LANES] for k in range(tiles)], axis=0
-                )
-                packed[part, pair, color] = both.astype(jnp.bfloat16)
-                if part == 0:
-                    packed[2, pair, color] = (-both).astype(jnp.bfloat16)
+            turned[pair, color] = -narrow(0, *divmod(pair, SPINS), color)
 
     def row(a, carry):
         def load(part, pair):
-            return [packed[part, pair, color].astype(jnp.float32) for color in range(spread)]
+            s1, s2 = pair >> 2, pair & 3
+            return [narrow(part, s1, s2, color).astype(jnp.float32) for color in range(spread)]
 
         def total(left, right):
             acc = left[0] * right[0]
@@ -105,11 +104,12 @@
             return acc
 
         def put(d, value):
-            start = pl.multiple_of((a * PAIRS + d) * rows_x, rows_x)
+            start = (a * PAIRS + d) * (rows_x + 1)
             for tile in range(tiles):
                 gram[tile, pl.ds(start, rows_x), :] = value[tile * rows_x : (tile + 1) * rows_x]
 
-        ar, ai, an = load(0, a), load(1, a), load(2, a)
+        ar, ai = load(0, a), load(1, a)
+        an = [turned[a, color].astype(jnp.float32) for color in range(spread)]
         put(0, total(ar + ai, ar + ai))
         for d in range(1, PAIRS // 2 + 1):
             b = (a + d) & (PAIRS - 1)
@@ -122,24 +122,24 @@
                 put(d, jnp.where(a < PAIRS // 2, real, imag))
         return carry
 
-    lax.fori_loop(0, PAIRS, row, 0)
+    lax.fori_loop(0, PAIRS, row, 0, unroll=2)
 
     pieces = []
     for tile in range(tiles):
         for x in range(rows_x):
-            products = gram[tile, pl.ds(x, SLOTS, stride=rows_x), :].astype(jnp.bfloat16)
+            products = gram[tile, pl.ds(x, SLOTS, stride=rows_x + 1), :].astype(jnp.bfloat16)
             dens = jnp.dot(weights[...], products, preferred_element_type=jnp.float32)
             dens = dens.astype(jnp.bfloat16)
             pieces.append(jnp.concatenate([dens[:channels], dens[channels:]], axis=1))
     stacked = jnp.concatenate(pieces, axis=0)
-    turned = lax.dot_general(
+    spread_z = lax.dot_general(
         zmat[...], stacked, (((1,), (1,)), ((), ())), preferred_element_type=jnp.float32
     )
     width = rows_x * channels
-    rows = turned.shape[0] // owners
-    turned = turned.reshape(owners, rows, tiles * width)
+    rows = spread_z.shape[0] // owners
+    spread_z = spread_z.reshape(owners, rows, tiles * width)
     out[0] = jnp.concatenate(
-        [turned[:, :, k * width : (k + 1) * width] for k in range(tiles)], axis=1
+        [spread_z[:, :, k * width : (k + 1) * width] for k in range(tiles)], axis=1
     ).astype(jnp.bfloat16)
 
 
@@ -207,8 +207,8 @@
         out_shape=jax.ShapeDtypeStruct((slices, owners, rows, width), jnp.bfloat16),
         scratch_shapes=[
             pltpu.VMEM((2 * channels, SLOTS), jnp.bfloat16),
-            pltpu.VMEM((3, PAIRS, colors * colors, tiles * rows_x, LANES), jnp.bfloat16),
-            pltpu.VMEM((tiles, SLOTS * rows_x, LANES), jnp.float32),
+            pltpu.VMEM((PAIRS, colors * colors, tiles * rows_x, LANES), jnp.bfloat16),
+            pltpu.VMEM((tiles, SLOTS * (rows_x + 1), LANES), jnp.float32),
         ],
         name="front",
     )(propagator, gamma_table.T, zmat)

time: 36.2 us -> 34.7 us (0.959)
  Pallas kernels: 13.5 us -> 12 us
    pallas_call x1, Pallas kernels: 10.4 us -> 8.92 us  [body(): pl.pallas_call(functools.partial(front_kernel, tiles=tiles, colors=colors...]
where the time goes in v3:
time: 34.7 us; the launch traced here: 34.4 us
  blocking collectives  22.5 us (65%)
  Pallas kernels  12 us (35%)
    all_to_all x1, blocking collectives, body(): lax.all_to_all(sent, ('gx', 'gy'), split_axis=1, concat_axis=1, tiled=True)  22.5 us
    pallas_call x1, Pallas kernels, body(): pl.pallas_call(functools.partial(front_kernel, tiles=tiles, colors=colors...  8.92 us
    pallas_call x1, Pallas kernels, body(): pl.pallas_call(functools.partial(back_kernel, grid_x=grid_x, rows_x=rows_...  3.03 us

profile of v3, /device:TPU:1, one launch (start us, length us, event | category | flops | bytes accessed | tf_op | source)
XLA Modules:
  0.0 34.4 jit_solution(5890526990757271667)
XLA Ops:
  0.0 8.9 %front.1 = bf16[1,32,64,128]{3,2,1,0:T(8,128)(2,1)} custom-call(bf16[1,2,4,3,4,3,8,1024]{7,6,5,4,3,2,1,0:T(8,128)(2,1)} %prop.1, s32[8,16]{1,0:T(8,128)} %bitcast.5, bf16[256,256]{1,0:T(8,128)(2,1)} %constant.6.clone.zmat), custom_call_target="tpu_custom_call" | custom-call | tf_op jit(solution)/shard_map/front/pallas_call | solution.py:193
  8.9 22.5 %all_to_all.5 = bf16[1,32,64,128]{3,2,0,1:T(8,128)(2,1)} all-to-all(bf16[1,32,64,128]{3,2,0,1:T(8,128)(2,1)} %bitcast.4), channel_id=1, replica_groups=mesh['ta'=1,'gx'=8,'gy'=4] {'gx','gy'}, dimensions={1} | all-to-all | bytes 1048576 | tf_op jit(solution)/shard_map/all_to_all | solution.py:216
  31.4 3.0 %back.1 = f32[1,16,2,64,128]{4,3,2,1,0:T(8,128)} custom-call(bf16[1,8,256,128]{3,2,1,0:T(8,128)(2,1)} %bitcast.3, bf16[256,512]{1,0:T(8,128)(2,1)} %constant.7.clone.ymat, bf16[64,128]{1,0:T(8,128)(2,1)} %constant.8.clone.xmat), custom_call_target="tpu_custom_call" | custom-call | tf_op jit(solution)/shard_map/back/pallas_call | solution.py:220
